TPU v7x, 32 devices: a whole 2x2x4 slice. The times are simulated.
32 devices in a mesh: grp: 8 (over y, x, core), col: 4 (over z).
Axes of the slice: x: 2, y: 2, z: 4, core: 2. Of those that a mesh axis runs over, the one named last changes fastest.
Arguments:
- old_tables: bfloat16 [32, 128, 32768], P(('grp', 'col')), may hold values from -3 to 3
- table_rows: int32 [32], replicated, may hold values from 4096 to 32768, as said below
- old_plan: int32 [32], replicated, may hold values from 0 to 31, each once
- new_plan: int32 [32], replicated, may hold values from 0 to 31, each once
- ids: int32 [256, 32, 16], P(('grp', 'col')), may hold values from 0 to 32767, as said below
- bag_len: int32 [256, 32], P(('grp', 'col')), may hold values from 1 to 16
Outputs:
- new_tables: bfloat16 [32, 128, 32768], P('grp', 'col')
- pooled: float32 [256, 32, 128], P(('grp', 'col'))
Inputs may be any that keep to these rules, and one draw needn't show every extreme that they name: table_rows[t] is a multiple of 4096, and some table has exactly 32768 rows. `ids`: every id of table t lies below table_rows[t].
All inputs are finite; a program needn't handle non-finite values.
Results may differ from a plain program's by a relative error of at most 0.001.
Values may be sent and summed in bfloat16 or wider, within the bound.
A program may use at most 128 MiB of HBM per device.

v0:
```python
import jax
import jax.numpy as jnp
from jax import lax
from jax.sharding import PartitionSpec as P


def invert(permutation):
    entries = permutation.shape[0]
    across = lax.broadcasted_iota(jnp.int32, (entries, entries), 1)
    down = lax.broadcasted_iota(jnp.int32, (entries, entries), 0)
    return jnp.sum(jnp.where(permutation[None, :] == down, across, 0), axis=1)


def pool_rows(table_cols, marked):
    columns = table_cols.shape[0]
    safe_ids = jnp.maximum(marked, 0).reshape(-1)
    weights = (marked >= 0).astype(jnp.float32)
    picked = (
        jnp.take(table_cols, safe_ids, axis=1)
        .reshape(columns, marked.shape[0], marked.shape[1])
        .astype(jnp.float32)
    )
    return jnp.sum(picked * weights[None, :, :], axis=2)


def reorder_blocks(spread, source_rows):
    count = spread.shape[0]
    across = lax.broadcasted_iota(jnp.int32, (count, count), 1)
    selector = (source_rows[:, None] == across).astype(spread.dtype)
    flat = spread.reshape(count, -1)
    picked = jnp.dot(selector, flat, preferred_element_type=jnp.float32).astype(spread.dtype)
    return picked.reshape(spread.shape)


def body(old_tables, table_rows, old_plan, new_plan, ids, bag_len):
    group_count = lax.axis_size("grp")
    col_count = lax.axis_size("col")
    device_count = group_count * col_count
    full_width = old_tables.shape[1]
    table_len = old_tables.shape[2]
    row_block = table_len // device_count
    narrow = full_width // col_count
    per_group = new_plan.shape[0] // group_count
    bag_size = ids.shape[2]
    own_slot = lax.axis_index("grp") * col_count + lax.axis_index("col")
    own_table = old_plan[own_slot]
    row_limit = table_rows[own_table]
    row_iota = lax.broadcasted_iota(jnp.int32, (1, table_len), 1)
    owned_table = old_tables[0] * (row_iota < row_limit).astype(old_tables.dtype)
    spread = lax.all_to_all(
        owned_table.reshape(full_width, device_count, row_block),
        ("grp", "col"),
        split_axis=1,
        concat_axis=0,
        tiled=True,
    )
    spread = spread.reshape(device_count * col_count, narrow, row_block)
    old_inverse = invert(old_plan)
    source_slot = old_inverse[new_plan].reshape(group_count, 1, per_group)
    source_rows = (
        source_slot * col_count + lax.broadcasted_iota(jnp.int32, (1, col_count, 1), 1)
    ).reshape(-1)
    blocks = reorder_blocks(spread, source_rows)
    direct = lax.all_to_all(
        blocks.reshape(device_count, per_group, narrow, row_block),
        ("grp", "col"),
        split_axis=0,
        concat_axis=3,
        tiled=True,
    )
    new_local = direct.reshape(per_group, narrow, table_len)
    bag_iota = lax.broadcasted_iota(jnp.int32, (1, 1, bag_size), 2)
    marked = jnp.where(bag_iota < bag_len[:, :, None], ids, -1)
    by_slot = jnp.take(marked, old_plan, axis=1)
    own_ids = lax.all_to_all(
        by_slot, ("grp", "col"), split_axis=1, concat_axis=0, tiled=True
    ).reshape(-1, bag_size)
    partial_value = pool_rows(owned_table, own_ids)
    returned = lax.all_to_all(
        partial_value.reshape(1, full_width, -1),
        ("grp", "col"),
        split_axis=2,
        concat_axis=0,
        tiled=True,
    )
    by_table = jnp.take(returned, old_inverse, axis=0)
    pooled = jnp.transpose(by_table, (2, 0, 1))
    return (new_local, pooled)


def solution(mesh):
    return jax.shard_map(
        body,
        mesh=mesh,
        in_specs=(
            P(("grp", "col"), None, None),
            P(),
            P(),
            P(),
            P(("grp", "col"), None, None),
            P(("grp", "col"), None),
        ),
        out_specs=(P("grp", "col", None), P(("grp", "col"), None, None)),
        check_vma=False,
    )
```

profile of v0, /device:TPU:9, one launch (start us, length us, event | category | flops | bytes accessed | tf_op | source)
XLA Modules:
  0.0 492.5 jit_solution(5518799861332294195)
XLA Ops:
  0.6 0.7 compare_select_fusion.1
  1.3 0.7 compare_and_fusion
  2.0 0.9 copy.25
  2.9 0.8 copy.24
  3.8 0.6 gather_fusion.1
  4.5 0.7 reshape.168
  5.2 6.3 %all-to-all-start.2 = ((s32[32,1,128]{2,1,0:T(1,128)}), s32[32,1,128]{2,1,0:T(1,128)S(1)}, u32[]{:S(2)}, u32[]{:S(2)}) async-start(s32[32,1,128]{2,1,0:T(1,128)} %reshape.168), calls=%async_computation.2 | async-start | bytes 32768 | tf_op jit(solution)/shard_map/all_to_all | solution.py:75
  11.5 1.2 dynamic_slice.6
  14.7 1.3 dynamic_slice.7
  16.0 0.7 fusion
  16.7 12.4 %copy.28 = bf16[16,8,32,1024]{3,2,1,0:T(8,128)(2,1)} copy(bf16[16,8,32,1024]{3,1,2,0:T(8,128)(2,1)} %bitcast.70) | data formatting | bytes 16777216
  29.1 16.0 %copy_multiply_fusion = bf16[128,32,1024]{2,0,1:T(8,128)(2,1)} fusion(bf16[128,32,1024]{2,1,0:T(8,128)(2,1)} %bitcast.72, bf16[32,1024]{1,0:T(8,128)(2,1)S(1)} %fusion), kind=kLoop, calls=%fused_computation.6 | loop fusion | flops 4194304 | bytes 16842752 | tf_op jit(solution)/shard_map/mul | solution.py:49
  45.1 5.9 %all-to-all-start = ((bf16[128,32,1024]{2,0,1:T(8,128)(2,1)}), bf16[128,32,1024]{2,0,1:T(8,128)(2,1)}, u32[]{:S(2)}, u32[]{:S(2)}) async-start(bf16[128,32,1024]{2,0,1:T(8,128)(2,1)} %copy_multiply_fusion), calls=%async_computation | async-start | bytes 16777216 | tf_op jit(solution)/shard_map/all_to_all | solution.py:50
  51.0 11.9 %copy.26 = bf16[1,128,32768]{1,2,0:T(8,128)(2,1)} copy(bf16[1,128,32768]{2,1,0:T(8,128)(2,1)} %param.6) | data formatting | bytes 16777216 | tf_op args[0]
  63.0 0.7 gather_fusion
  64.0 0.7 fusion.2
  64.6 8.6 %bitcast_multiply_fusion = bf16[128,32768]{0,1:T(8,128)(2,1)} fusion(bf16[1,128,32768]{1,2,0:T(8,128)(2,1)} %copy.26, bf16[32768]{0:T(1024)(128)(2,1)S(1)} %fusion.2), kind=kLoop, calls=%fused_computation.5 | loop fusion | flops 4194304 | bytes 16842752 | tf_op jit(solution)/shard_map/mul | solution.py:49
  73.2 0.5 broadcast.144
  73.7 0.7 reduce
  74.6 15.5 %gather_fusion.2 = bf16[4096,128]{1,0:T(8,128)(2,1)S(1)} fusion(bf16[128,32768]{0,1:T(8,128)(2,1)} %bitcast_multiply_fusion, s32[4096]{0:T(1024)S(1)} %broadcast_clamp_fusion), kind=kCustom, calls=%fused_computation.2 | custom fusion | bytes 2113536 | tf_op jit(solution)/shard_map/jit(_take)/gather | solution.py:19
  90.1 2.2 multiply_reduce_fusion
  92.3 144.8 %all-to-all-done = bf16[128,32,1024]{2,0,1:T(8,128)(2,1)} async-done(((bf16[128,32,1024]{2,0,1:T(8,128)(2,1)}), bf16[128,32,1024]{2,0,1:T(8,128)(2,1)}, u32[]{:S(2)}, u32[]{:S(2)}) %all-to-all-start) | async-done | bytes 8388640 | tf_op jit(solution)/shard_map/all_to_all | solution.py:50
  237.1 3.7 all-to-all-start.3
  240.8 13.4 %reshape_reshape.6 = bf16[128,32768]{1,0:T(8,128)(2,1)} reshape(bf16[32,128,1,1024]{3,1,0,2:T(8,128)(2,1)} %bitcast.3) | data formatting | bytes 16777216 | tf_op jit(solution)/shard_map/reshape;reshape | solution.py:30
  254.2 9.0 %convolution_convert_fusion = bf16[128,32768]{1,0:T(8,128)(2,1)} fusion(bf16[128,32768]{1,0:T(8,128)(2,1)} %reshape_reshape.6, s32[128]{0:T(128)S(1)} %add.73), kind=kOutput, calls=%fused_computation.4 | convolution fusion | flops 1077952512 | bytes 16777728 | tf_op jit(solution)/shard_map/dot_general | solution.py:31
  263.2 12.4 %copy.29 = bf16[16,8,32,1024]{3,2,1,0:T(8,128)(2,1)} copy(bf16[16,8,32,1024]{3,1,2,0:T(8,128)(2,1)} %bitcast.69) | data formatting | bytes 16777216
  275.6 5.9 %all-to-all-start.1 = ((bf16[32,4,32,1024]{3,2,1,0:T(8,128)(2,1)}), bf16[32,4,32,1024]{3,2,1,0:T(8,128)(2,1)}, u32[]{:S(2)}, u32[]{:S(2)}) async-start(bf16[32,4,32,1024]{3,2,1,0:T(8,128)(2,1)} %bitcast.71), calls=%async_computation.1 | async-start | bytes 16777216 | tf_op jit(solution)/shard_map/all_to_all | solution.py:64
  281.6 0.6 gather_fusion.3
  282.3 0.7 copy.27
  282.9 184.7 %all-to-all-done.1 = bf16[32,4,32,1024]{3,2,1,0:T(8,128)(2,1)} async-done(((bf16[32,4,32,1024]{3,2,1,0:T(8,128)(2,1)}), bf16[32,4,32,1024]{3,2,1,0:T(8,128)(2,1)}, u32[]{:S(2)}, u32[]{:S(2)}) %all-to-all-start.1) | async-done | bytes 8388640 | tf_op jit(solution)/shard_map/all_to_all | solution.py:64
  467.7 11.4 %copy.23 = bf16[1,4,32,32,1024]{4,3,2,1,0:T(8,128)(2,1)} copy(bf16[1,4,32,32,1024]{4,2,1,3,0:T(8,128)(2,1)} %bitcast.5) | data formatting | bytes 16777216 | tf_op jit(solution)/shard_map/all_to_all | solution.py:64
  479.1 13.4 %reshape.129 = bf16[4,32,32768]{2,1,0:T(8,128)(2,1)} reshape(bf16[1,4,32,32,1024]{4,3,2,1,0:T(8,128)(2,1)} %copy.23) | data formatting | bytes 16777216 | tf_op jit(solution)/shard_map/reshape | solution.py:71
  (25 shorter events, 0.9 us)
Async XLA Ops:
  5.2 39.9 %all-to-all-start.2 = ((s32[32,1,128]{2,1,0:T(1,128)}), s32[32,1,128]{2,1,0:T(1,128)S(1)}, u32[]{:S(2)}, u32[]{:S(2)}) async-start(s32[32,1,128]{2,1,0:T(1,128)} %reshape.168), calls=%async_computation.2 | async-start | bytes 32768 | tf_op jit(solution)/shard_map/all_to_all | solution.py:75
  45.1 192.0 %all-to-all-start = ((bf16[128,32,1024]{2,0,1:T(8,128)(2,1)}), bf16[128,32,1024]{2,0,1:T(8,128)(2,1)}, u32[]{:S(2)}, u32[]{:S(2)}) async-start(bf16[128,32,1024]{2,0,1:T(8,128)(2,1)} %copy_multiply_fusion), calls=%async_computation | async-start | bytes 16777216 | tf_op jit(solution)/shard_map/all_to_all | solution.py:50
  51.0 11.9 %copy-start = (s32[32]{0:T(128)S(1)}, s32[32]{0:T(128)}, u32[]{:S(2)}) copy-start(s32[32]{0:T(128)} %param.9) | copy-start | bytes 388
  51.0 11.9 %copy-start.1 = (s32[32]{0:T(128)S(1)}, s32[32]{0:T(128)}, u32[]{:S(2)}) copy-start(s32[32]{0:T(128)} %param.8) | copy-start | bytes 388
  237.1 38.5 %all-to-all-start.3 = ((f32[1,128,256]{1,0,2:T(1,128)}), f32[1,128,256]{1,0,2:T(1,128)S(1)}, u32[]{:S(2)}, u32[]{:S(2)}) async-start(f32[1,128,256]{1,0,2:T(1,128)} %bitcast.18), calls=%async_computation.3 | async-start | bytes 262144 | tf_op jit(solution)/shard_map/all_to_all | solution.py:79
  275.6 192.0 %all-to-all-start.1 = ((bf16[32,4,32,1024]{3,2,1,0:T(8,128)(2,1)}), bf16[32,4,32,1024]{3,2,1,0:T(8,128)(2,1)}, u32[]{:S(2)}, u32[]{:S(2)}) async-start(bf16[32,4,32,1024]{3,2,1,0:T(8,128)(2,1)} %bitcast.71), calls=%async_computation.1 | async-start | bytes 16777216 | tf_op jit(solution)/shard_map/all_to_all | solution.py:64
where the time goes:
time: 494 us; the launch traced here: 492 us
  waiting for transfers between devices  329 us (67%)
  local copies, waits for them, and re-layouts  98.9 us (20%)
  other arithmetic  30.6 us (6%)
  starting transfers between devices  21.8 us (4%)
  matrix products  8.98 us (2%)
    all_to_all x1, waiting for transfers between devices, body(): lax.all_to_all(blocks.reshape(device_count, per_group, narrow, row_block)...  185 us
    all_to_all x1, waiting for transfers between devices, body(): lax.all_to_all(owned_table.reshape(full_width, device_count, row_block),...  145 us
    unnamed x12, local copies, waits for them, and re-layouts  39.9 us
    mul x2, other arithmetic, body(): old_tables[0] * (row_iota < row_limit).astype(old_tables.dtype)  24.6 us
    gather x1, local copies, waits for them, and re-layouts, pool_rows(): jnp.take(table_cols, safe_ids, axis=1)  15.5 us
    another operation x1, local copies, waits for them, and re-layouts, reorder_blocks(): flat = spread.reshape(count, -1)  13.4 us
    reshape x1, local copies, waits for them, and re-layouts, body(): new_local = direct.reshape(per_group, narrow, table_len)  13.4 us
    all_to_all x1, local copies, waits for them, and re-layouts, body(): lax.all_to_all(blocks.reshape(device_count, per_group, narrow, row_block)...  11.4 us
  transfers between devices with their start and end apart: 4, of which 2 were waited for; matrix products, arithmetic and copies ran while one was open for 22% of the time, Pallas kernels for 0%

commit v1 on v0

v1 whole, which is shorter than its diff:
```python
import functools

import jax
import jax.numpy as jnp
from jax import lax
from jax.experimental import pallas as pl
from jax.experimental.pallas import tpu as pltpu
from jax.sharding import PartitionSpec as P

MESH = pl.DeviceIdType.MESH


def invert(permutation):
    entries = permutation.shape[0]
    across = lax.broadcasted_iota(jnp.int32, (entries, entries), 1)
    down = lax.broadcasted_iota(jnp.int32, (entries, entries), 0)
    return jnp.sum(jnp.where(permutation[None, :] == down, across, 0), axis=1)


def pool_rows(table_cols, marked):
    columns = table_cols.shape[0]
    safe_ids = jnp.maximum(marked, 0).reshape(-1)
    weights = (marked >= 0).astype(jnp.float32)
    picked = (
        jnp.take(table_cols, safe_ids, axis=1)
        .reshape(columns, marked.shape[0], marked.shape[1])
        .astype(jnp.float32)
    )
    return jnp.sum(picked * weights[None, :, :], axis=2)


def move_kernel(groups, cols, chunks, source_ref, table_ref, out_ref, *scratch):
    zbufs, spreads, picks = scratch[:chunks], scratch[chunks : 2 * chunks], scratch[2 * chunks : 3 * chunks]
    z_send, z_recv, s_send, s_recv, p_send, p_recv = scratch[3 * chunks :]
    g = lax.axis_index("grp")
    c = lax.axis_index("col")
    per_group, narrow, table_len = out_ref.shape
    chunk_rows = table_len // chunks
    sub = chunk_rows // groups

    def aligned(value, unit):
        return pl.multiple_of(value * unit, unit)

    def column_step(k, d):
        to = lax.rem(c + d, cols)
        src = table_ref.at[0, pl.ds(aligned(to, narrow), narrow), pl.ds(k * chunk_rows, chunk_rows)]
        dst = zbufs[k].at[c]
        if d == 0:
            return pltpu.make_async_copy(src, dst, z_recv.at[k, d])
        return pltpu.make_async_remote_copy(
            src, dst, z_send.at[k, d], z_recv.at[k, d], device_id=(g, to), device_id_type=MESH
        )

    def spread_step(k, d):
        to = lax.rem(g + d, groups)
        src = zbufs[k].at[:, :, pl.ds(aligned(to, sub), sub)]
        dst = spreads[k].at[pl.ds(g * cols, cols)]
        if d == 0:
            return pltpu.make_async_copy(src, dst, s_recv.at[k, d])
        return pltpu.make_async_remote_copy(
            src, dst, s_send.at[k, d], s_recv.at[k, d], device_id=(to, c), device_id_type=MESH
        )

    def group_step(k, d):
        to = lax.rem(g + d, groups)
        src = picks[k].at[pl.ds(to * per_group, per_group)]
        dst = out_ref.at[:, :, pl.ds(aligned(k * groups + g, sub), sub)]
        if d == 0:
            return pltpu.make_async_copy(src, dst, p_recv.at[k, d])
        return pltpu.make_async_remote_copy(
            src, dst, p_send.at[k, d], p_recv.at[k, d], device_id=(to, c), device_id_type=MESH
        )

    def finish(copy, d):
        if d == 0:
            copy.wait()
        else:
            copy.wait_recv()

    col_order = [d for d in (2, 1, 3) if d < cols] + list(range(4, cols)) + [0]
    grp_order = list(range(1, groups)) + [0]

    for k in range(chunks):
        for d in col_order:
            column_step(k, d).start()

    def route(k):
        for d in grp_order:
            finish(spread_step(k, d), d)

        def pick(i, carry):
            picks[k][i] = spreads[k][source_ref[i]]
            return carry

        lax.fori_loop(0, groups * per_group, pick, 0)
        for d in grp_order:
            group_step(k, d).start()

    for k in range(chunks):
        for d in col_order:
            finish(column_step(k, d), d)
        for d in grp_order:
            spread_step(k, d).start()
        if k > 0:
            route(k - 1)
    route(chunks - 1)
    for k in range(chunks):
        for d in grp_order:
            finish(group_step(k, d), d)
        for d in col_order:
            if d > 0:
                column_step(k, d).wait_send()
        for d in grp_order:
            if d > 0:
                spread_step(k, d).wait_send()
                group_step(k, d).wait_send()


def move_tables(old_tables, source_slot, groups, cols):
    _, width, table_len = old_tables.shape
    narrow = width // cols
    tables = source_slot.shape[0]
    per_group = tables // groups
    chunks = min(8, table_len // (groups * 128))
    chunk_rows = table_len // chunks
    sub = chunk_rows // groups
    dtype = old_tables.dtype
    sems = [
        pltpu.SemaphoreType.DMA((chunks, n)) for n in (cols, cols, groups, groups, groups, groups)
    ]
    return pl.pallas_call(
        functools.partial(move_kernel, groups, cols, chunks),
        out_shape=jax.ShapeDtypeStruct((per_group, narrow, table_len), dtype),
        in_specs=[
            pl.BlockSpec(memory_space=pltpu.SMEM),
            pl.BlockSpec(memory_space=pl.ANY),
        ],
        out_specs=pl.BlockSpec(memory_space=pl.ANY),
        scratch_shapes=[pltpu.VMEM((cols, narrow, chunk_rows), dtype)] * chunks
        + [pltpu.VMEM((groups * cols, narrow, sub), dtype)] * chunks
        + [pltpu.VMEM((tables, narrow, sub), dtype)] * chunks
        + sems,
        compiler_params=pltpu.CompilerParams(
            has_side_effects=True, vmem_limit_bytes=48 * 1024 * 1024
        ),
    )(source_slot, old_tables)


def body(old_tables, table_rows, old_plan, new_plan, ids, bag_len):
    group_count = lax.axis_size("grp")
    col_count = lax.axis_size("col")
    full_width = old_tables.shape[1]
    table_len = old_tables.shape[2]
    per_group = new_plan.shape[0] // group_count
    bag_size = ids.shape[2]
    old_inverse = invert(old_plan)
    moved = move_tables(old_tables, old_inverse[new_plan], group_count, col_count)
    new_ids = lax.dynamic_slice_in_dim(new_plan, lax.axis_index("grp") * per_group, per_group)
    limits = table_rows[new_ids]
    row_iota = lax.broadcasted_iota(jnp.int32, (1, 1, table_len), 2)
    new_local = jnp.where(row_iota < limits[:, None, None], moved, jnp.zeros((), moved.dtype))
    bag_iota = lax.broadcasted_iota(jnp.int32, (1, 1, bag_size), 2)
    marked = jnp.where(bag_iota < bag_len[:, :, None], ids, -1)
    by_slot = jnp.take(marked, old_plan, axis=1)
    own_ids = lax.all_to_all(
        by_slot, ("grp", "col"), split_axis=1, concat_axis=0, tiled=True
    ).reshape(-1, bag_size)
    partial_value = pool_rows(old_tables[0], own_ids)
    returned = lax.all_to_all(
        partial_value.reshape(1, full_width, -1),
        ("grp", "col"),
        split_axis=2,
        concat_axis=0,
        tiled=True,
    )
    by_table = jnp.take(returned, old_inverse, axis=0)
    pooled = jnp.transpose(by_table, (2, 0, 1))
    return (new_local, pooled)


def solution(mesh):
    return jax.shard_map(
        body,
        mesh=mesh,
        in_specs=(
            P(("grp", "col"), None, None),
            P(),
            P(),
            P(),
            P(("grp", "col"), None, None),
            P(("grp", "col"), None),
        ),
        out_specs=(P("grp", "col", None), P(("grp", "col"), None, None)),
        check_vma=False,
    )
```

time: 494 us -> 342 us (0.69)
  waiting for transfers between devices: 329 us -> 6.76 us
  Pallas kernels: 0 us -> 273 us
  local copies, waits for them, and re-layouts: 98.9 us -> 33.7 us
  other arithmetic: 30.6 us -> 15.7 us
  starting transfers between devices: 21.8 us -> 9.12 us
  matrix products: 8.98 us -> 0 us
    all_to_all x2 -> x0, waiting for transfers between devices: 329 us -> none  [the longest x1 185 us: body(): lax.all_to_all(blocks.reshape(device_count, per_group, narrow, row_block)...]
    pallas_call x0 -> x1, Pallas kernels: none -> 273 us  [move_tables(): pl.pallas_call(functools.partial(move_kernel, groups, cols, chunks), out_...]
    unnamed x12 -> x8, local copies, waits for them, and re-layouts: 39.9 us -> 15.1 us
    mul x3 -> x0, other arithmetic: 24.6 us -> none  [the longest x2 24.6 us: body(): old_tables[0] * (row_iota < row_limit).astype(old_tables.dtype)]
    another operation x1 -> x0, local copies, waits for them, and re-layouts: 13.4 us -> none  [reorder_blocks(): flat = spread.reshape(count, -1)]
    reshape x1 -> x0, local copies, waits for them, and re-layouts: 13.4 us -> none  [body(): new_local = direct.reshape(per_group, narrow, table_len)]
    all_to_all x2 -> x0, starting transfers between devices: 11.8 us -> none  [the longest x1 5.9 us: body(): lax.all_to_all(blocks.reshape(device_count, per_group, narrow, row_block)...]
    all_to_all x1 -> x0, local copies, waits for them, and re-layouts: 11.4 us -> none  [body(): lax.all_to_all(blocks.reshape(device_count, per_group, narrow, row_block)...]
  transfers between devices with their start and end apart: 4 -> 2, of which waited for: 2 -> 1; matrix products, arithmetic and copies ran while one was open for 22% -> 7% of each run, Pallas kernels for 0% -> 80%
where the time goes in v1:
time: 342 us; the launch traced here: 339 us
  Pallas kernels  273 us (80%)
  local copies, waits for them, and re-layouts  33.7 us (10%)
  other arithmetic  15.7 us (5%)
  starting transfers between devices  9.12 us (3%)
  waiting for transfers between devices  6.76 us (2%)
    pallas_call x1, Pallas kernels, move_tables(): pl.pallas_call(functools.partial(move_kernel, groups, cols, chunks), out_...  273 us
    gather x1, local copies, waits for them, and re-layouts, pool_rows(): jnp.take(table_cols, safe_ids, axis=1)  15.5 us
    unnamed x8, local copies, waits for them, and re-layouts  15.1 us
    select_n x1, other arithmetic, body(): jnp.where(row_iota < limits[:, None, None], moved, jnp.zeros((), moved.dt...  8.72 us
  transfers between devices with their start and end apart: 2, of which 1 were waited for; matrix products, arithmetic and copies ran while one was open for 7% of the time, Pallas kernels for 80%

profile of v1, /device:TPU:9, one launch (start us, length us, event | category | flops | bytes accessed | tf_op | source)
XLA Modules:
  0.0 338.7 jit_solution(12467304341145873621)
XLA Ops:
  0.6 0.0 copy-start
  0.6 0.7 compare_select_fusion.1
  1.3 0.7 compare_and_fusion
  2.0 0.9 copy.18
  2.9 0.8 copy.17
  3.7 0.1 fusion
  3.8 0.6 gather_fusion.2
  4.4 0.1 fusion.2
  4.5 0.7 reshape.153
  5.2 6.3 %all-to-all-start = ((s32[32,1,128]{2,1,0:T(1,128)}), s32[32,1,128]{2,1,0:T(1,128)S(1)}, u32[]{:S(2)}, u32[]{:S(2)}) async-start(s32[32,1,128]{2,1,0:T(1,128)} %reshape.153), calls=%async_computation | async-start | bytes 32768 | tf_op jit(solution)/shard_map/all_to_all | solution.py:165
  11.6 0.8 select_reduce_fusion
  12.3 0.7 compare_select_fusion.3
  13.0 0.7 compare_select_fusion.4
  13.7 0.0 copy-done
  13.7 0.6 gather_fusion
  14.4 0.2 iota_compare_fusion
  14.6 0.7 gather_fusion.1
  15.3 272.5 %shard_map.77 = bf16[4,32,32768]{2,1,0:T(8,128)(2,1)} custom-call(s32[32]{0:T(128)S(1)} %gather_fusion.1, bf16[1,128,32768]{2,1,0:T(8,128)(2,1)} %table_ref.1), custom_call_target="tpu_custom_call" | custom-call | tf_op jit(solution)/shard_map/pallas_call | solution.py:131
  287.9 8.7 %broadcast_select_fusion = bf16[4,32,32768]{2,1,0:T(8,128)(2,1)} fusion(bf16[4,32,32768]{2,1,0:T(8,128)(2,1)} %shard_map.77, pred[4,32768]{1,0:T(4,128)(4,1)S(1)} %iota_compare_fusion), kind=kLoop, calls=%fused_computation.5 | loop fusion | flops 4194304 | bytes 16908288 | tf_op jit(solution)/shard_map/jit(_where)/select_n | solution.py:161
  296.6 11.9 %copy.19 = bf16[1,128,32768]{1,2,0:T(8,128)(2,1)} copy(bf16[1,128,32768]{2,1,0:T(8,128)(2,1)} %table_ref.1) | data formatting | bytes 16777216 | tf_op args[0]
  308.5 0.0 all-to-all-done
  308.5 0.5 broadcast.150
  309.0 0.7 reduce
  309.7 0.1 reshape.154
  309.9 0.1 reshape.135
  310.0 15.5 %gather_fusion.3 = bf16[4096,128]{1,0:T(8,128)(2,1)S(1)} fusion(bf16[128,32768]{0,1:T(8,128)(2,1)} %bitcast.47, s32[4096]{0:T(1024)S(1)} %broadcast_clamp_fusion), kind=kCustom, calls=%fused_computation.3 | custom fusion | bytes 2113536 | tf_op jit(solution)/shard_map/jit(_take)/gather | solution.py:25
  325.5 2.2 multiply_reduce_fusion
  327.7 2.8 all-to-all-start.1
  330.5 6.8 %all-to-all-done.1 = f32[1,128,256]{1,0,2:T(1,128)S(1)} async-done(((f32[1,128,256]{1,0,2:T(1,128)}), f32[1,128,256]{1,0,2:T(1,128)S(1)}, u32[]{:S(2)}, u32[]{:S(2)}) %all-to-all-start.1) | async-done | bytes 131104 | tf_op jit(solution)/shard_map/all_to_all | solution.py:169
  337.3 0.6 gather_fusion.4
  337.9 0.1 select_bitcast_fusion.1
  338.0 0.7 copy.20
  (9 shorter events, 0.1 us)
Async XLA Ops:
  0.6 13.1 %copy-start = (s32[32]{0:T(128)S(1)}, s32[32]{0:T(128)}, u32[]{:S(2)}) copy-start(s32[32]{0:T(128)} %param.7) | copy-start | bytes 388
  5.2 303.3 %all-to-all-start = ((s32[32,1,128]{2,1,0:T(1,128)}), s32[32,1,128]{2,1,0:T(1,128)S(1)}, u32[]{:S(2)}, u32[]{:S(2)}) async-start(s32[32,1,128]{2,1,0:T(1,128)} %reshape.153), calls=%async_computation | async-start | bytes 32768 | tf_op jit(solution)/shard_map/all_to_all | solution.py:165
  327.7 9.6 %all-to-all-start.1 = ((f32[1,128,256]{1,0,2:T(1,128)}), f32[1,128,256]{1,0,2:T(1,128)S(1)}, u32[]{:S(2)}, u32[]{:S(2)}) async-start(f32[1,128,256]{1,0,2:T(1,128)} %bitcast.12), calls=%async_computation.1 | async-start | bytes 262144 | tf_op jit(solution)/shard_map/all_to_all | solution.py:169

commit v2 on v1

--- a/solution.py
+++ b/solution.py
@@ -7,6 +7,8 @@
 from jax.experimental.pallas import tpu as pltpu
 from jax.sharding import PartitionSpec as P
 
+WINDOW = 2
+CHUNKS = 16
 MESH = pl.DeviceIdType.MESH
 
 
@@ -17,21 +19,10 @@
     return jnp.sum(jnp.where(permutation[None, :] == down, across, 0), axis=1)
 
 
-def pool_rows(table_cols, marked):
-    columns = table_cols.shape[0]
-    safe_ids = jnp.maximum(marked, 0).reshape(-1)
-    weights = (marked >= 0).astype(jnp.float32)
-    picked = (
-        jnp.take(table_cols, safe_ids, axis=1)
-        .reshape(columns, marked.shape[0], marked.shape[1])
-        .astype(jnp.float32)
-    )
-    return jnp.sum(picked * weights[None, :, :], axis=2)
-
-
-def move_kernel(groups, cols, chunks, source_ref, table_ref, out_ref, *scratch):
+def move_kernel(groups, cols, chunks, source_ref, table_ref, ids_ref, out_ref, sums_ref, *scratch):
     zbufs, spreads, picks = scratch[:chunks], scratch[chunks : 2 * chunks], scratch[2 * chunks : 3 * chunks]
-    z_send, z_recv, s_send, s_recv, p_send, p_recv = scratch[3 * chunks :]
+    z_send, z_recv, s_send, s_recv, p_send, p_recv = scratch[3 * chunks : 3 * chunks + 6]
+    own_ids, tabs, total, i_send, i_recv, r_send, r_recv, t_sem = scratch[3 * chunks + 6 :]
     g = lax.axis_index("grp")
     c = lax.axis_index("col")
     per_group, narrow, table_len = out_ref.shape
@@ -71,6 +62,70 @@
             src, dst, p_send.at[k, d], p_recv.at[k, d], device_id=(to, c), device_id_type=MESH
         )
 
+    devices = groups * cols
+    me = g * cols + c
+    samples, bag = ids_ref.shape[1:]
+
+    def ids_step(d):
+        to = lax.rem(me + d, devices)
+        src, dst = ids_ref.at[to], own_ids.at[me]
+        if isinstance(d, int):
+            return pltpu.make_async_copy(src, dst, i_recv.at[d])
+        return pltpu.make_async_remote_copy(
+            src, dst, i_send.at[d], i_recv.at[d],
+            device_id=(to // cols, lax.rem(to, cols)), device_id_type=MESH,
+        )
+
+    def sums_step(d):
+        to = lax.rem(me + d, devices)
+        src, dst = total.at[to], sums_ref.at[me]
+        if isinstance(d, int):
+            return pltpu.make_async_copy(src, dst, r_recv.at[d])
+        return pltpu.make_async_remote_copy(
+            src, dst, r_send.at[d], r_recv.at[d],
+            device_id=(to // cols, lax.rem(to, cols)), device_id_type=MESH,
+        )
+
+    def each_peer(act):
+        def step(d, carry):
+            act(d)
+            return carry
+
+        lax.fori_loop(1, devices, step, 0)
+
+    def fetch(k):
+        return pltpu.make_async_copy(
+            table_ref.at[0, :, pl.ds(k * chunk_rows, chunk_rows)], tabs.at[k % 2], t_sem.at[k % 2]
+        )
+
+    tile = 512 if chunk_rows % 512 == 0 else 128
+    fold = 8 if devices % 8 == 0 else 1
+
+    def pool(k):
+        fetch(k).wait()
+        if k + 1 < chunks:
+            fetch(k + 1).start()
+        columns = chunk_rows // tile
+
+        def piece(step, carry):
+            block, part = step // columns, lax.rem(step, columns)
+            rows = samples * fold
+            wanted = own_ids[pl.ds(block * fold, fold)].reshape(rows, bag)
+            row = lax.broadcasted_iota(jnp.int32, (rows, tile), 1) + (k * chunk_rows + part * tile)
+            counts = jnp.zeros((rows, tile), jnp.float32)
+            for i in range(bag):
+                counts = jnp.where(wanted[:, i : i + 1] == row, counts + 1.0, counts)
+            values = tabs[k % 2, :, pl.ds(aligned(part, tile), tile)]
+            sums = lax.dot_general(
+                counts.astype(values.dtype), values, (((1,), (1,)), ((), ())),
+                preferred_element_type=jnp.float32,
+            )
+            where = pl.ds(block * fold, fold)
+            total[where] = total[where] + sums.reshape(fold, samples, values.shape[0])
+            return carry
+
+        lax.fori_loop(0, devices // fold * columns, piece, 0)
+
     def finish(copy, d):
         if d == 0:
             copy.wait()
@@ -80,9 +135,15 @@
     col_order = [d for d in (2, 1, 3) if d < cols] + list(range(4, cols)) + [0]
     grp_order = list(range(1, groups)) + [0]
 
-    for k in range(chunks):
+    each_peer(lambda d: ids_step(d).start())
+    ids_step(0).start()
+    fetch(0).start()
+    for k in range(min(WINDOW, chunks)):
         for d in col_order:
             column_step(k, d).start()
+    total[...] = jnp.zeros_like(total)
+    each_peer(lambda d: ids_step(d).wait_recv())
+    ids_step(0).wait()
 
     def route(k):
         for d in grp_order:
@@ -101,8 +162,14 @@
             finish(column_step(k, d), d)
         for d in grp_order:
             spread_step(k, d).start()
+        if k + WINDOW < chunks:
+            for d in col_order:
+                column_step(k + WINDOW, d).start()
         if k > 0:
             route(k - 1)
+        pool(k)
+    each_peer(lambda d: sums_step(d).start())
+    sums_step(0).start()
     route(chunks - 1)
     for k in range(chunks):
         for d in grp_order:
@@ -114,67 +181,69 @@
             if d > 0:
                 spread_step(k, d).wait_send()
                 group_step(k, d).wait_send()
-
-
-def move_tables(old_tables, source_slot, groups, cols):
+    each_peer(lambda d: ids_step(d).wait_send())
+    each_peer(lambda d: sums_step(d).wait())
+    sums_step(0).wait()
+
+
+def move_tables(old_tables, source_slot, by_slot, groups, cols):
     _, width, table_len = old_tables.shape
     narrow = width // cols
     tables = source_slot.shape[0]
     per_group = tables // groups
-    chunks = min(8, table_len // (groups * 128))
+    chunks = min(CHUNKS, table_len // (groups * 128))
     chunk_rows = table_len // chunks
     sub = chunk_rows // groups
     dtype = old_tables.dtype
+    devices, samples, _ = by_slot.shape
     sems = [
         pltpu.SemaphoreType.DMA((chunks, n)) for n in (cols, cols, groups, groups, groups, groups)
     ]
     return pl.pallas_call(
         functools.partial(move_kernel, groups, cols, chunks),
-        out_shape=jax.ShapeDtypeStruct((per_group, narrow, table_len), dtype),
+        out_shape=(
+            jax.ShapeDtypeStruct((per_group, narrow, table_len), dtype),
+            jax.ShapeDtypeStruct((devices, samples, width), jnp.float32),
+        ),
         in_specs=[
             pl.BlockSpec(memory_space=pltpu.SMEM),
             pl.BlockSpec(memory_space=pl.ANY),
+            pl.BlockSpec(memory_space=pltpu.VMEM),
         ],
-        out_specs=pl.BlockSpec(memory_space=pl.ANY),
+        out_specs=(pl.BlockSpec(memory_space=pl.ANY), pl.BlockSpec(memory_space=pltpu.VMEM)),
         scratch_shapes=[pltpu.VMEM((cols, narrow, chunk_rows), dtype)] * chunks
         + [pltpu.VMEM((groups * cols, narrow, sub), dtype)] * chunks
         + [pltpu.VMEM((tables, narrow, sub), dtype)] * chunks
-        + sems,
+        + sems
+        + [
+            pltpu.VMEM(by_slot.shape, by_slot.dtype),
+            pltpu.VMEM((2, width, chunk_rows), dtype),
+            pltpu.VMEM((devices, samples, width), jnp.float32),
+        ]
+        + [pltpu.SemaphoreType.DMA((devices,))] * 4
+        + [pltpu.SemaphoreType.DMA((2,))],
         compiler_params=pltpu.CompilerParams(
             has_side_effects=True, vmem_limit_bytes=48 * 1024 * 1024
         ),
-    )(source_slot, old_tables)
+    )(source_slot, old_tables, by_slot)
 
 
 def body(old_tables, table_rows, old_plan, new_plan, ids, bag_len):
     group_count = lax.axis_size("grp")
     col_count = lax.axis_size("col")
-    full_width = old_tables.shape[1]
     table_len = old_tables.shape[2]
     per_group = new_plan.shape[0] // group_count
     bag_size = ids.shape[2]
     old_inverse = invert(old_plan)
-    moved = move_tables(old_tables, old_inverse[new_plan], group_count, col_count)
+    bag_iota = lax.broadcasted_iota(jnp.int32, (1, 1, bag_size), 2)
+    marked = jnp.where(bag_iota < bag_len[:, :, None], ids, -1)
+    by_slot = jnp.transpose(jnp.take(marked, old_plan, axis=1), (1, 0, 2))
+    moved, sums = move_tables(old_tables, old_inverse[new_plan], by_slot, group_count, col_count)
     new_ids = lax.dynamic_slice_in_dim(new_plan, lax.axis_index("grp") * per_group, per_group)
     limits = table_rows[new_ids]
     row_iota = lax.broadcasted_iota(jnp.int32, (1, 1, table_len), 2)
     new_local = jnp.where(row_iota < limits[:, None, None], moved, jnp.zeros((), moved.dtype))
-    bag_iota = lax.broadcasted_iota(jnp.int32, (1, 1, bag_size), 2)
-    marked = jnp.where(bag_iota < bag_len[:, :, None], ids, -1)
-    by_slot = jnp.take(marked, old_plan, axis=1)
-    own_ids = lax.all_to_all(
-        by_slot, ("grp", "col"), split_axis=1, concat_axis=0, tiled=True
-    ).reshape(-1, bag_size)
-    partial_value = pool_rows(old_tables[0], own_ids)
-    returned = lax.all_to_all(
-        partial_value.reshape(1, full_width, -1),
-        ("grp", "col"),
-        split_axis=2,
-        concat_axis=0,
-        tiled=True,
-    )
-    by_table = jnp.take(returned, old_inverse, axis=0)
-    pooled = jnp.transpose(by_table, (2, 0, 1))
+    pooled = jnp.transpose(jnp.take(sums, old_inverse, axis=0), (1, 0, 2))
     return (new_local, pooled)
 
 

time: 342 us -> 250 us (0.73)
  Pallas kernels: 273 us -> 231 us
  local copies, waits for them, and re-layouts: 33.7 us -> 4.91 us
  starting transfers between devices: 9.12 us -> 0 us
  waiting for transfers between devices: 6.76 us -> 0 us
    pallas_call x1, Pallas kernels: 273 us -> 231 us  [move_tables(): pl.pallas_call(functools.partial(move_kernel, groups, cols, chunks), out_...]
    gather x3 -> x2, local copies, waits for them, and re-layouts: 16.7 us -> 1.17 us  [the longest x1 0.58 us: body(): pooled = jnp.transpose(jnp.take(sums, old_inverse, axis=0), (1, 0, 2))]
    unnamed x8 -> x5, local copies, waits for them, and re-layouts: 15.1 us -> 2.41 us
    all_to_all x2 -> x0, starting transfers between devices: 9.12 us -> none  [the longest x1 6.32 us: body(): lax.all_to_all(by_slot, ('grp', 'col'), split_axis=1, concat_axis=0, tile...]
    all_to_all x2 -> x0, waiting for transfers between devices: 6.76 us -> none  [the longest x1 6.76 us: body(): lax.all_to_all(partial_value.reshape(1, full_width, -1), ('grp', 'col'),...]
  transfers between devices with their start and end apart: 2 -> 0, of which waited for: 1 -> 0; matrix products, arithmetic and copies ran while one was open for 7% -> 0% of each run, Pallas kernels for 80% -> 0%
where the time goes in v2:
time: 250 us; the launch traced here: 249 us
  Pallas kernels  231 us (92%)
  other arithmetic  12.8 us (5%)
  local copies, waits for them, and re-layouts  4.91 us (2%)
    pallas_call x1, Pallas kernels, move_tables(): pl.pallas_call(functools.partial(move_kernel, groups, cols, chunks), out_...  231 us
    select_n x1, other arithmetic, body(): jnp.where(row_iota < limits[:, None, None], moved, jnp.zeros((), moved.dt...  8.72 us

profile of v2, /device:TPU:9, one launch (start us, length us, event | category | flops | bytes accessed | tf_op | source)
XLA Modules:
  0.0 249.4 jit_solution(11734633205773111657)
XLA Ops:
  0.6 0.0 copy-start
  0.6 0.7 compare_select_fusion.4
  1.4 0.0 copy-done
  1.4 0.6 gather_fusion
  2.0 0.2 iota_compare_fusion
  2.3 0.8 select_reduce_fusion
  3.0 0.7 compare_select_fusion.3
  3.7 0.7 gather_fusion.1
  4.4 1.0 copy.13
  5.4 0.8 copy.12
  6.1 0.1 fusion
  6.2 0.7 compare_select_fusion.2
  6.9 0.6 gather_fusion.2
  7.5 0.7 compare_and_fusion.1
  8.2 0.1 broadcast_select_fusion.1.ids_ref
  8.3 231.0 %shard_map.77 = (bf16[4,32,32768]{2,1,0:T(8,128)(2,1)}, f32[32,8,128]{2,1,0:T(8,128)S(1)}) custom-call(s32[32]{0:T(128)S(1)} %gather_fusion.1, bf16[1,128,32768]{2,1,0:T(8,128)(2,1)} %table_ref.1, s32[32,8,16]{2,1,0:T(8,128)S(1)} %broadcast_select_fusion.1.ids_ref), custom_call_target="tpu_custom_call" | custom-call | tf_op jit(solution)/shard_map/pallas_call | solution.py:202
  239.3 8.7 %broadcast_select_fusion = bf16[4,32,32768]{2,1,0:T(8,128)(2,1)} fusion(bf16[4,32,32768]{2,1,0:T(8,128)(2,1)} %get-tuple-element.4, pred[4,32768]{1,0:T(4,128)(4,1)S(1)} %iota_compare_fusion), kind=kLoop, calls=%fused_computation.4 | loop fusion | flops 4194304 | bytes 16908288 | tf_op jit(solution)/shard_map/jit(_where)/select_n | solution.py:245
  248.0 0.6 gather_fusion.3
  248.6 0.1 select_bitcast_fusion
  248.7 0.7 copy.14
  (6 shorter events, 0.0 us)
Async XLA Ops:
  0.6 0.8 copy-start

commit v3 on v2

--- a/solution.py
+++ b/solution.py
@@ -8,21 +8,16 @@
 from jax.sharding import PartitionSpec as P
 
 WINDOW = 2
-CHUNKS = 16
+CHUNKS = 32
+ORDER = (4, 2, 6, 3, 5, 7, 1)
 MESH = pl.DeviceIdType.MESH
 
 
-def invert(permutation):
-    entries = permutation.shape[0]
-    across = lax.broadcasted_iota(jnp.int32, (entries, entries), 1)
-    down = lax.broadcasted_iota(jnp.int32, (entries, entries), 0)
-    return jnp.sum(jnp.where(permutation[None, :] == down, across, 0), axis=1)
-
-
-def move_kernel(groups, cols, chunks, source_ref, table_ref, ids_ref, out_ref, sums_ref, *scratch):
+def move_kernel(groups, cols, chunks, old_ref, new_ref, table_ref, ids_ref, out_ref, pooled_ref, *scratch):
     zbufs, spreads, picks = scratch[:chunks], scratch[chunks : 2 * chunks], scratch[2 * chunks : 3 * chunks]
     z_send, z_recv, s_send, s_recv, p_send, p_recv = scratch[3 * chunks : 3 * chunks + 6]
-    own_ids, tabs, total, i_send, i_recv, r_send, r_recv, t_sem = scratch[3 * chunks + 6 :]
+    own_ids, by_slot, tabs, total, sums_ref, source_ref, inverse_ref = scratch[3 * chunks + 6 : 3 * chunks + 13]
+    i_send, i_recv, r_send, r_recv, t_sem = scratch[3 * chunks + 13 :]
     g = lax.axis_index("grp")
     c = lax.axis_index("col")
     per_group, narrow, table_len = out_ref.shape
@@ -64,11 +59,11 @@
 
     devices = groups * cols
     me = g * cols + c
-    samples, bag = ids_ref.shape[1:]
+    samples, tables, bag = ids_ref.shape
 
     def ids_step(d):
         to = lax.rem(me + d, devices)
-        src, dst = ids_ref.at[to], own_ids.at[me]
+        src, dst = by_slot.at[to], own_ids.at[me]
         if isinstance(d, int):
             return pltpu.make_async_copy(src, dst, i_recv.at[d])
         return pltpu.make_async_remote_copy(
@@ -133,14 +128,30 @@
             copy.wait_recv()
 
     col_order = [d for d in (2, 1, 3) if d < cols] + list(range(4, cols)) + [0]
-    grp_order = list(range(1, groups)) + [0]
-
-    each_peer(lambda d: ids_step(d).start())
-    ids_step(0).start()
-    fetch(0).start()
+    grp_order = [d for d in ORDER if d < groups] + list(range(8, groups)) + [0]
+
+    def order_ids(s, carry):
+        by_slot[s] = ids_ref[:, pl.ds(old_ref[s], 1), :].reshape(samples, bag)
+        return carry
+
+    def locate(j, carry):
+        wanted = new_ref[j]
+
+        def look(s, found):
+            held = old_ref[s]
+            return jnp.where(held == wanted, s, found[0]), jnp.where(held == j, s, found[1])
+
+        source_ref[j], inverse_ref[j] = lax.fori_loop(0, tables, look, (0, 0))
+        return carry
+
     for k in range(min(WINDOW, chunks)):
         for d in col_order:
             column_step(k, d).start()
+    fetch(0).start()
+    lax.fori_loop(0, tables, order_ids, 0)
+    lax.fori_loop(0, tables, locate, 0)
+    each_peer(lambda d: ids_step(d).start())
+    ids_step(0).start()
     total[...] = jnp.zeros_like(total)
     each_peer(lambda d: ids_step(d).wait_recv())
     ids_step(0).wait()
@@ -168,9 +179,9 @@
         if k > 0:
             route(k - 1)
         pool(k)
+    route(chunks - 1)
     each_peer(lambda d: sums_step(d).start())
     sums_step(0).start()
-    route(chunks - 1)
     for k in range(chunks):
         for d in grp_order:
             finish(group_step(k, d), d)
@@ -184,18 +195,21 @@
     each_peer(lambda d: ids_step(d).wait_send())
     each_peer(lambda d: sums_step(d).wait())
     sums_step(0).wait()
-
-
-def move_tables(old_tables, source_slot, by_slot, groups, cols):
+    for t in range(tables):
+        pooled_ref[:, t, :] = sums_ref[inverse_ref[t]]
+
+
+def move_tables(old_tables, old_plan, new_plan, marked, groups, cols):
     _, width, table_len = old_tables.shape
     narrow = width // cols
-    tables = source_slot.shape[0]
+    tables = old_plan.shape[0]
     per_group = tables // groups
     chunks = min(CHUNKS, table_len // (groups * 128))
     chunk_rows = table_len // chunks
     sub = chunk_rows // groups
     dtype = old_tables.dtype
-    devices, samples, _ = by_slot.shape
+    devices = groups * cols
+    samples, _, bag = marked.shape
     sems = [
         pltpu.SemaphoreType.DMA((chunks, n)) for n in (cols, cols, groups, groups, groups, groups)
     ]
@@ -203,9 +217,10 @@
         functools.partial(move_kernel, groups, cols, chunks),
         out_shape=(
             jax.ShapeDtypeStruct((per_group, narrow, table_len), dtype),
-            jax.ShapeDtypeStruct((devices, samples, width), jnp.float32),
+            jax.ShapeDtypeStruct((samples, tables, width), jnp.float32),
         ),
         in_specs=[
+            pl.BlockSpec(memory_space=pltpu.SMEM),
             pl.BlockSpec(memory_space=pltpu.SMEM),
             pl.BlockSpec(memory_space=pl.ANY),
             pl.BlockSpec(memory_space=pltpu.VMEM),
@@ -216,35 +231,56 @@
         + [pltpu.VMEM((tables, narrow, sub), dtype)] * chunks
         + sems
         + [
-            pltpu.VMEM(by_slot.shape, by_slot.dtype),
+            pltpu.VMEM((devices, samples, bag), marked.dtype),
+            pltpu.VMEM((devices, samples, bag), marked.dtype),
             pltpu.VMEM((2, width, chunk_rows), dtype),
             pltpu.VMEM((devices, samples, width), jnp.float32),
+            pltpu.VMEM((devices, samples, width), jnp.float32),
+            pltpu.SMEM((tables,), jnp.int32),
+            pltpu.SMEM((tables,), jnp.int32),
         ]
         + [pltpu.SemaphoreType.DMA((devices,))] * 4
         + [pltpu.SemaphoreType.DMA((2,))],
         compiler_params=pltpu.CompilerParams(
             has_side_effects=True, vmem_limit_bytes=48 * 1024 * 1024
         ),
-    )(source_slot, old_tables, by_slot)
+    )(old_plan, new_plan, old_tables, marked)
+
+
+def clear_kernel(per_group, step, plan_ref, rows_ref, moved_ref, out_ref):
+    own = lax.axis_index("grp") * per_group + pl.program_id(0)
+    limit = rows_ref[plan_ref[own]] - pl.program_id(1) * step
+    row = lax.broadcasted_iota(jnp.int32, moved_ref.shape, 2)
+    out_ref[...] = jnp.where(row < limit, moved_ref[...], jnp.zeros_like(moved_ref))
+
+
+def clear_unused(moved, new_plan, table_rows):
+    per_group, narrow, table_len = moved.shape
+    step = min(8192, table_len)
+
+    def source(p, r, plan_ref, rows_ref):
+        own = lax.axis_index("grp") * per_group + p
+        return p, 0, jnp.minimum(r, (rows_ref[plan_ref[own]] - 1) // step)
+
+    return pl.pallas_call(
+        functools.partial(clear_kernel, per_group, step),
+        out_shape=jax.ShapeDtypeStruct(moved.shape, moved.dtype),
+        grid_spec=pltpu.PrefetchScalarGridSpec(
+            num_scalar_prefetch=2,
+            grid=(per_group, table_len // step),
+            in_specs=[pl.BlockSpec((1, narrow, step), source)],
+            out_specs=pl.BlockSpec((1, narrow, step), lambda p, r, *_: (p, 0, r)),
+        ),
+    )(new_plan, table_rows, moved)
 
 
 def body(old_tables, table_rows, old_plan, new_plan, ids, bag_len):
     group_count = lax.axis_size("grp")
     col_count = lax.axis_size("col")
-    table_len = old_tables.shape[2]
-    per_group = new_plan.shape[0] // group_count
-    bag_size = ids.shape[2]
-    old_inverse = invert(old_plan)
-    bag_iota = lax.broadcasted_iota(jnp.int32, (1, 1, bag_size), 2)
+    bag_iota = lax.broadcasted_iota(jnp.int32, (1, 1, ids.shape[2]), 2)
     marked = jnp.where(bag_iota < bag_len[:, :, None], ids, -1)
-    by_slot = jnp.transpose(jnp.take(marked, old_plan, axis=1), (1, 0, 2))
-    moved, sums = move_tables(old_tables, old_inverse[new_plan], by_slot, group_count, col_count)
-    new_ids = lax.dynamic_slice_in_dim(new_plan, lax.axis_index("grp") * per_group, per_group)
-    limits = table_rows[new_ids]
-    row_iota = lax.broadcasted_iota(jnp.int32, (1, 1, table_len), 2)
-    new_local = jnp.where(row_iota < limits[:, None, None], moved, jnp.zeros((), moved.dtype))
-    pooled = jnp.transpose(jnp.take(sums, old_inverse, axis=0), (1, 0, 2))
-    return (new_local, pooled)
+    moved, pooled = move_tables(old_tables, old_plan, new_plan, marked, group_count, col_count)
+    return (clear_unused(moved, new_plan, table_rows), pooled)
 
 
 def solution(mesh):

time: 250 us -> 242 us (0.968)
  other arithmetic: 12.8 us -> 0.79 us
  Pallas kernels: 231 us -> 236 us
    pallas_call x0 -> x1, Pallas kernels: none -> 11.4 us  [clear_unused(): pl.pallas_call(functools.partial(clear_kernel, per_group, step), out_shap...]
    select_n x7 -> x0, other arithmetic: 11 us -> none  [the longest x1 8.72 us: body(): jnp.where(row_iota < limits[:, None, None], moved, jnp.zeros((), moved.dt...]
    pallas_call x1, Pallas kernels: 231 us -> 224 us  [move_tables(): pl.pallas_call(functools.partial(move_kernel, groups, cols, chunks), out_...]
    gather x4 -> x0, local copies, waits for them, and re-layouts: 2.5 us -> none  [the longest x1 0.7 us: body(): old_inverse[new_plan]]
where the time goes in v3:
time: 242 us; the launch traced here: 240 us
  Pallas kernels  236 us (98%)
  local copies, waits for them, and re-layouts  2.89 us (1%)
    pallas_call x1, Pallas kernels, move_tables(): pl.pallas_call(functools.partial(move_kernel, groups, cols, chunks), out_...  224 us
    pallas_call x1, Pallas kernels, clear_unused(): pl.pallas_call(functools.partial(clear_kernel, per_group, step), out_shap...  11.4 us

profile of v3, /device:TPU:9, one launch (start us, length us, event | category | flops | bytes accessed | tf_op | source)
XLA Modules:
  0.0 240.0 jit_solution(8127745655580744193)
XLA Ops:
  0.6 0.9 copy.8
  1.6 0.8 fusion.ids_ref
  2.4 0.0 copy-start
  2.4 0.6 copy-done
  3.0 0.0 copy-start.1
  3.0 0.7 copy-done.1
  3.7 224.3 %shard_map.77 = (bf16[4,32,32768]{2,1,0:T(8,128)(2,1)}, f32[8,32,128]{2,1,0:T(8,128)S(1)}) custom-call(s32[32]{0:T(128)S(1)} %copy-done.1, s32[32]{0:T(128)S(1)} %copy-done, bf16[1,128,32768]{2,1,0:T(8,128)(2,1)} %table_ref.1, s32[8,32,16]{2,1,0:T(8,128)S(1)} %fusion.ids_ref), custom_call_target="tpu_custom_call" | custom-call | tf_op jit(solution)/shard_map/pallas_call | solution.py:216
  228.0 11.4 %shard_map.78 = bf16[4,32,32768]{2,1,0:T(8,128)(2,1)} custom-call(s32[32]{0:T(128)} %plan_ref.1, s32[32]{0:T(128)} %rows_ref.1, bf16[4,32,32768]{2,1,0:T(8,128)(2,1)} %get-tuple-element.4.moved_ref), custom_call_target="tpu_custom_call" | custom-call | tf_op jit(solution)/shard_map/pallas_call | solution.py:265
  239.4 0.7 copy.10
Async XLA Ops:
  2.4 0.7 copy-start
  3.0 0.7 copy-start.1

commit v4 on v3

--- a/solution.py
+++ b/solution.py
@@ -137,11 +137,13 @@
     def locate(j, carry):
         wanted = new_ref[j]
 
-        def look(s, found):
+        source, inverse = jnp.int32(0), jnp.int32(0)
+        for s in range(1, tables):
             held = old_ref[s]
-            return jnp.where(held == wanted, s, found[0]), jnp.where(held == j, s, found[1])
-
-        source_ref[j], inverse_ref[j] = lax.fori_loop(0, tables, look, (0, 0))
+            source = jnp.where(held == wanted, s, source)
+            inverse = jnp.where(held == j, s, inverse)
+        source_ref[j] = source
+        inverse_ref[j] = inverse
         return carry
 
     for k in range(min(WINDOW, chunks)):
@@ -153,8 +155,6 @@
     each_peer(lambda d: ids_step(d).start())
     ids_step(0).start()
     total[...] = jnp.zeros_like(total)
-    each_peer(lambda d: ids_step(d).wait_recv())
-    ids_step(0).wait()
 
     def route(k):
         for d in grp_order:
@@ -178,10 +178,15 @@
                 column_step(k + WINDOW, d).start()
         if k > 0:
             route(k - 1)
-        pool(k)
-    route(chunks - 1)
+        if k == 0:
+            each_peer(lambda d: ids_step(d).wait_recv())
+            ids_step(0).wait()
+            pool(0)
+        if k + 1 < chunks:
+            pool(k + 1)
     each_peer(lambda d: sums_step(d).start())
     sums_step(0).start()
+    route(chunks - 1)
     for k in range(chunks):
         for d in grp_order:
             finish(group_step(k, d), d)
@@ -247,40 +252,17 @@
     )(old_plan, new_plan, old_tables, marked)
 
 
-def clear_kernel(per_group, step, plan_ref, rows_ref, moved_ref, out_ref):
-    own = lax.axis_index("grp") * per_group + pl.program_id(0)
-    limit = rows_ref[plan_ref[own]] - pl.program_id(1) * step
-    row = lax.broadcasted_iota(jnp.int32, moved_ref.shape, 2)
-    out_ref[...] = jnp.where(row < limit, moved_ref[...], jnp.zeros_like(moved_ref))
-
-
-def clear_unused(moved, new_plan, table_rows):
-    per_group, narrow, table_len = moved.shape
-    step = min(8192, table_len)
-
-    def source(p, r, plan_ref, rows_ref):
-        own = lax.axis_index("grp") * per_group + p
-        return p, 0, jnp.minimum(r, (rows_ref[plan_ref[own]] - 1) // step)
-
-    return pl.pallas_call(
-        functools.partial(clear_kernel, per_group, step),
-        out_shape=jax.ShapeDtypeStruct(moved.shape, moved.dtype),
-        grid_spec=pltpu.PrefetchScalarGridSpec(
-            num_scalar_prefetch=2,
-            grid=(per_group, table_len // step),
-            in_specs=[pl.BlockSpec((1, narrow, step), source)],
-            out_specs=pl.BlockSpec((1, narrow, step), lambda p, r, *_: (p, 0, r)),
-        ),
-    )(new_plan, table_rows, moved)
-
-
 def body(old_tables, table_rows, old_plan, new_plan, ids, bag_len):
     group_count = lax.axis_size("grp")
     col_count = lax.axis_size("col")
     bag_iota = lax.broadcasted_iota(jnp.int32, (1, 1, ids.shape[2]), 2)
     marked = jnp.where(bag_iota < bag_len[:, :, None], ids, -1)
     moved, pooled = move_tables(old_tables, old_plan, new_plan, marked, group_count, col_count)
-    return (clear_unused(moved, new_plan, table_rows), pooled)
+    per_group = moved.shape[0]
+    own = lax.dynamic_slice_in_dim(new_plan, lax.axis_index("grp") * per_group, per_group)
+    row = lax.broadcasted_iota(jnp.int32, (1, 1, moved.shape[2]), 2)
+    used = row < table_rows[own][:, None, None]
+    return (jnp.where(used, moved, jnp.zeros((), moved.dtype)), pooled)
 
 
 def solution(mesh):

time: 242 us -> 245 us (1.012)
  other arithmetic: 0.79 us -> 10.5 us
  Pallas kernels: 236 us -> 228 us
    pallas_call x1 -> x0, Pallas kernels: 11.4 us -> none  [clear_unused(): pl.pallas_call(functools.partial(clear_kernel, per_group, step), out_shap...]
    select_n x0 -> x2, other arithmetic: none -> 9.46 us  [the longest x1 8.73 us: body(): return (jnp.where(used, moved, jnp.zeros((), moved.dtype)), pooled)]
    pallas_call x1, Pallas kernels: 224 us -> 228 us  [move_tables(): pl.pallas_call(functools.partial(move_kernel, groups, cols, chunks), out_...]
where the time goes in v4:
time: 245 us; the launch traced here: 243 us
  Pallas kernels  228 us (93%)
  other arithmetic  10.5 us (4%)
  local copies, waits for them, and re-layouts  3.54 us (1%)
    pallas_call x1, Pallas kernels, move_tables(): pl.pallas_call(functools.partial(move_kernel, groups, cols, chunks), out_...  228 us
    select_n x1, other arithmetic, body(): return (jnp.where(used, moved, jnp.zeros((), moved.dtype)), pooled)  8.73 us

profile of v4, /device:TPU:9, one launch (start us, length us, event | category | flops | bytes accessed | tf_op | source)
XLA Modules:
  0.0 242.7 jit_solution(4626421039482558153)
XLA Ops:
  0.6 0.0 copy-start
  0.6 0.7 compare_select_fusion
  1.4 0.0 copy-done
  1.4 0.6 gather_fusion
  2.0 0.2 iota_compare_fusion
  2.3 0.9 copy.9
  3.2 0.8 fusion.ids_ref
  4.0 0.0 copy-start.1
  4.0 0.6 copy-done.1
  4.7 0.0 copy-start.2
  4.7 0.7 copy-done.2
  5.3 227.9 %shard_map.77 = (bf16[4,32,32768]{2,1,0:T(8,128)(2,1)}, f32[8,32,128]{2,1,0:T(8,128)S(1)}) custom-call(s32[32]{0:T(128)S(1)} %copy-done.1, s32[32]{0:T(128)S(1)} %copy-done.2, bf16[1,128,32768]{2,1,0:T(8,128)(2,1)} %table_ref.1, s32[8,32,16]{2,1,0:T(8,128)S(1)} %fusion.ids_ref), custom_call_target="tpu_custom_call" | custom-call | tf_op jit(solution)/shard_map/pallas_call | solution.py:221
  233.3 8.7 %broadcast_select_fusion = bf16[4,32,32768]{2,1,0:T(8,128)(2,1)} fusion(bf16[4,32,32768]{2,1,0:T(8,128)(2,1)} %get-tuple-element.4, pred[4,32768]{1,0:T(4,128)(4,1)S(1)} %iota_compare_fusion), kind=kLoop, calls=%fused_computation.1 | loop fusion | flops 4194304 | bytes 16908288 | tf_op jit(solution)/shard_map/jit(_where)/select_n | solution.py:265
  242.0 0.7 copy.11
  (1 shorter events, 0.0 us)
Async XLA Ops:
  0.6 0.8 copy-start
  4.0 0.7 copy-start.1
  4.7 0.7 copy-start.2
